TPU v7x, 32 devices: a whole 2x2x4 slice. The times are simulated.
32 devices in a mesh: gx: 4 (over y, x), gy: 4 (over z), gz: 2 (over core).
Axes of the slice: x: 2, y: 2, z: 4, core: 2. Of those that a mesh axis runs over, the one named last changes fastest.
Arguments:
- residual_in: float32 [2, 4, 64, 64, 256], P(None, None, 'gx', 'gy', 'gz'), may hold values from -15 to 15
- reaction: float32 [4, 64, 64, 256], P(None, 'gx', 'gy', 'gz'), may hold values from 0.5 to 2
- transport: float32 [4, 64, 64, 256], P(None, 'gx', 'gy', 'gz'), may hold values from 0.2 to 1
- congestion: float32 [4, 64, 64, 256], P(None, 'gx', 'gy', 'gz'), may hold values from 0.5 to 1.5
Outputs:
- newton_update: float32 [2, 4, 64, 64, 256], P(None, None, 'gx', 'gy', 'gz')
All inputs are finite; a program needn't handle non-finite values.
Results may differ from a plain program's by a relative error of at most 0.0003.
Values sent between devices are 32-bit elements; how exact they have to be, the bound alone decides.
A program may use at most 128 MiB of HBM per device.

v0:
```python
import functools

import jax
import jax.numpy as jnp
from jax import lax
from jax.experimental import pallas as pl
from jax.experimental.pallas import tpu as pltpu
from jax.sharding import PartitionSpec as P

ITERS = 8
AXES = ("gx", "gy", "gz")
time_rate = 1.0
SCALE = 2.5
BACK = 1.0
PIVOT = 2.5e-3
PLANES = 2


def pair_index(row, column):
    return column * (column + 1) // 2 + row


def least_squares(columns, beta, steps):
    zero = jnp.zeros_like(beta)
    rotations = []
    target = [beta] + [zero] * steps
    upper = []
    for column_index in range(steps):
        column = list(columns[column_index])
        for place, (cosine, sine) in enumerate(rotations):
            upper_entry = cosine * column[place] + sine * column[place + 1]
            lower_entry = -sine * column[place] + cosine * column[place + 1]
            column[place], column[place + 1] = (upper_entry, lower_entry)
        radius = jnp.sqrt(column[column_index] ** 2 + column[column_index + 1] ** 2)
        inverse = 1.0 / radius
        cosine = column[column_index] * inverse
        sine = column[column_index + 1] * inverse
        column[column_index] = inverse
        rotations.append((cosine, sine))
        target[column_index], target[column_index + 1] = (
            cosine * target[column_index],
            -sine * target[column_index],
        )
        upper.append(column[: column_index + 1])
    solved = [None] * steps
    for row_index in range(steps - 1, -1, -1):
        accum = target[row_index]
        for later_index in range(steps - 1, row_index, -1):
            accum = accum - upper[later_index][row_index] * solved[later_index]
        solved[row_index] = accum * upper[row_index][row_index]
    return solved


def gram_solve(gram, steps):
    size = steps + 1
    work = {(i, j): gram(i, j) for j in range(size) for i in range(j + 1)}
    factor = {}
    worst = None
    for i in range(size):
        ratio = work[i, i] / gram(i, i)
        worst = ratio if worst is None else jnp.where(ratio > worst, worst, ratio)
        pivot = jnp.sqrt(work[i, i])
        inverse = 1.0 / pivot
        factor[i, i] = pivot
        for j in range(i + 1, size):
            factor[i, j] = work[i, j] * inverse
        for a in range(i + 1, size):
            for b in range(a, size):
                work[a, b] = work[a, b] - factor[i, a] * factor[i, b]
    columns = []
    for k in range(steps):
        column = []
        for i in range(k + 2):
            entry = -factor[i, k + 1] * (1.0 / SCALE)
            if i <= k:
                entry = entry + factor[i, k]
            if k > 0 and i <= k - 1:
                entry = entry - factor[i, k - 1] * (BACK / SCALE)
            column.append(entry)
        columns.append(column)
    return least_squares(columns, factor[0, 0], steps), worst


def kernel(
    levels, sizes, residual, reaction, transport, congestion, out, flag,
    basis, inv, weight, couple, search, xin, yout, yin, zout, zin,
    gram, splat, gsend, gall, insem, ssem, rsem, gssem, grsem,
):
    fields = 2 * levels
    nx, ny, nz = residual.shape[1:]
    total = sizes[0] * sizes[1] * sizes[2]
    index = [lax.axis_index(axis) for axis in AXES]
    me = (index[0] * sizes[1] + index[1]) * sizes[2] + index[2]
    lane = lax.broadcasted_iota(jnp.int32, (ny, nz), 1)
    sub = lax.broadcasted_iota(jnp.int32, (ny, nz), 0)

    loads = [
        pltpu.make_async_copy(src, dst, insem.at[place])
        for place, (src, dst) in enumerate(
            ((residual, basis.at[0]), (reaction, inv), (transport, weight), (congestion, couple))
        )
    ]
    for load in loads:
        load.start()

    for buffer in (xin, yin, zin):
        buffer[...] = jnp.zeros_like(buffer)
    gram[...] = jnp.zeros_like(gram)

    def ident(other):
        return (other // (sizes[1] * sizes[2]), (other // sizes[2]) % sizes[1], other % sizes[2])

    barrier = pltpu.get_barrier_semaphore()

    def greet(step, carry):
        pl.semaphore_signal(
            barrier, inc=1, device_id=ident((me + step) % total),
            device_id_type=pl.DeviceIdType.MESH,
        )
        return carry

    lax.fori_loop(1, total, greet, 0)

    def remote(axis, side, slot):
        if axis == 0:
            src, dst = search.at[slot, :, nx - 1 if side == 0 else 0], xin.at[slot, side]
        elif axis == 1:
            src, dst = yout.at[slot, side], yin.at[slot, side]
        else:
            src, dst = zout.at[slot, side], zin.at[slot, side]
        target = list(index)
        target[axis] = index[axis] + (1 if side == 0 else -1)
        return pltpu.make_async_remote_copy(
            src_ref=src, dst_ref=dst,
            send_sem=ssem.at[axis, side, slot], recv_sem=rsem.at[axis, side, slot],
            device_id=tuple(target), device_id_type=pl.DeviceIdType.MESH,
        )

    def sends(axis, side):
        return index[axis] < sizes[axis] - 1 if side == 0 else index[axis] > 0

    def receives(axis, side):
        return index[axis] > 0 if side == 0 else index[axis] < sizes[axis] - 1

    def start(axis, slot):
        odd = index[axis] % 2 == 1
        up, down = sends(axis, 0), sends(axis, 1)

        @pl.when(jnp.logical_and(odd, up))
        def _():
            remote(axis, 0, slot).start()

        @pl.when(down)
        def _():
            remote(axis, 1, slot).start()

        @pl.when(jnp.logical_and(jnp.logical_not(odd), up))
        def _():
            remote(axis, 0, slot).start()

    def wait_sent(axis, slot):
        for side in range(2):
            @pl.when(sends(axis, side))
            def _():
                remote(axis, side, slot).wait_send()

    def wait_received(axis, slot):
        for side in range(2):
            @pl.when(receives(axis, side))
            def _():
                remote(axis, side, slot).wait_recv()

    def precondition(x, vector):
        value, density = [None] * levels, [None] * levels
        carry = None
        for t in range(levels - 1, -1, -1):
            carry = vector[t] if carry is None else vector[t] + carry
            carry = carry * inv[t, x]
            value[t] = carry
        carry = None
        for t in range(levels):
            push = vector[levels + t] + (6.0 * weight[t, x]) * value[t]
            carry = push if carry is None else push + carry
            carry = carry * inv[t, x]
            density[t] = carry
        return value + density

    def publish(planes, vectors, slot, packs):
        high, low = packs
        founds = [precondition(x, vector) for x, vector in zip(planes, vectors)]
        for x, found in zip(planes, founds):
            for f in range(fields):
                place = x * fields + f
                turned = pltpu.roll(found[f], place, 1)
                high = jnp.where(lane == (place + nz - 1) % nz, turned, high)
                low = jnp.where(lane == place, turned, low)
        for x, found in zip(planes, founds):
            for f in range(fields):
                search[slot, f, x] = found[f]
                yout[slot, 0, f, pl.ds(x, 1), :] = found[f][ny - 1 : ny, :]
                yout[slot, 1, f, pl.ds(x, 1), :] = found[f][0:1, :]
        return high, low

    def spatial(k, slot, planes):
        founds = [spatial_plane(k, slot, *plane) for plane in planes]
        for (x, _, _), found in zip(planes, founds):
            for f in range(fields):
                basis[k + 1, f, x] = found[f]

    def spatial_plane(k, slot, x, xlow, xhigh):
        def around(f):
            center = search[slot, f, x]
            up = jnp.where(sub == 0, 0.0, pltpu.roll(center, 1, 0))
            down = jnp.where(sub == ny - 1, 0.0, pltpu.roll(center, ny - 1, 0))
            place = x * fields + f
            edge = jnp.where(lane == (place + nz - 1) % nz, zin[slot, 0], zin[slot, 1])
            edge = pltpu.roll(edge, (nz - place) % nz, 1)
            left = pltpu.roll(jnp.where(lane == nz - 1, edge, center), 1, 1)
            right = pltpu.roll(jnp.where(lane == 0, edge, center), nz - 1, 1)
            return ((xlow(f) + xhigh(f)) + (up + down)) + (left + right)

        found = [None] * fields
        for t in range(levels):
            value = around(t)
            density = around(levels + t) - weight[t, x] * value
            value = value + couple[t, x] * search[slot, levels + t, x]
            for f, item in ((t, value), (levels + t, density)):
                item = SCALE * item
                if k > 0:
                    item = item - BACK * basis[k - 1, f, x]
                found[f] = item
        return found

    def finish(x, k, slot):
        def rows(f):
            low, high = yin[slot, 0, f, pl.ds(x, 1), :], yin[slot, 1, f, pl.ds(x, 1), :]
            return SCALE * jnp.where(sub == 0, low, jnp.where(sub == ny - 1, high, 0.0))

        vector = [None] * fields
        for t in range(levels - 1, -1, -1):
            value = rows(t)
            density = rows(levels + t) - weight[t, x] * value
            for f, item in ((t, value), (levels + t, density)):
                vector[f] = basis[k + 1, f, x] + item
        return vector

    def dots(k):
        def step(x, accs):
            accs = list(accs)
            for f in range(fields):
                own = basis[k, f, x]
                for j in range(k + 1):
                    other = own if j == k else basis[j, f, x]
                    accs[j] = accs[j] + own * other
            return tuple(accs)

        zero = jnp.zeros((ny, nz), jnp.float32)
        accs = lax.fori_loop(0, nx, step, (zero,) * (k + 1))
        for j in range(k + 1):
            row = pair_index(j, k)
            gram[row : row + 1, :] = jnp.sum(accs[j], axis=0, keepdims=True)

    for load in loads:
        load.wait()

    def invert(x, carry):
        for t in range(levels):
            inv[t, x] = 1.0 / (time_rate + 6.0 + inv[t, x])
        return carry

    lax.fori_loop(0, nx, invert, 0)
    blank = jnp.zeros((ny, nz), jnp.float32)

    def first(x, packs):
        planes = [x * PLANES + place for place in range(PLANES)]
        vectors = [[basis[0, f, x] for f in range(fields)] for x in planes]
        return publish(planes, vectors, 0, packs)

    packs = lax.fori_loop(0, nx // PLANES, first, (blank, blank))
    zout[0, 0], zout[0, 1] = packs
    pl.semaphore_wait(barrier, total - 1)
    start(0, 0)
    start(1, 0)
    start(2, 0)

    for k in range(ITERS):
        slot, later = k % 2, (k + 1) % 2
        last = k == ITERS - 1
        dots(k)
        if k > 0:
            for axis in range(3):
                wait_sent(axis, later)
        wait_received(2, slot)

        def inner(step, carry):
            spatial(k, slot, [
                (
                    x,
                    lambda f, x=x: search[slot, f, x - 1],
                    lambda f, x=x: search[slot, f, x + 1],
                )
                for x in (1 + step * PLANES + place for place in range(PLANES))
            ])
            return carry

        lax.fori_loop(0, (nx - 2) // PLANES, inner, 0)
        wait_received(1, slot)

        def settle(planes, packs):
            vectors = [finish(x, k, slot) for x in planes]
            for x, vector in zip(planes, vectors):
                for f in range(fields):
                    basis[k + 1, f, x] = vector[f]
            return packs if last else publish(planes, vectors, later, packs)

        packs = lax.fori_loop(
            0, (nx - 2) // PLANES,
            lambda step, packs: settle(
                [1 + step * PLANES + place for place in range(PLANES)], packs
            ),
            (blank, blank),
        )
        wait_received(0, slot)
        spatial(k, slot, [
            (0, lambda f: xin[slot, 0, f], lambda f: search[slot, f, 1]),
            (nx - 1, lambda f: search[slot, f, nx - 2], lambda f: xin[slot, 1, f]),
        ])
        packs = settle([0, nx - 1], packs)
        if not last:
            zout[later, 0], zout[later, 1] = packs
            for axis in range(3):
                start(axis, later)

    dots(ITERS)
    for axis in range(3):
        wait_sent(axis, (ITERS - 1) % 2)

    local = jnp.sum(gram[...].T, axis=0, keepdims=True)
    gsend[...] = local
    gall[me] = local

    def spread(step, carry):
        pltpu.make_async_remote_copy(
            src_ref=gsend, dst_ref=gall.at[me], send_sem=gssem, recv_sem=grsem,
            device_id=ident((me + step) % total), device_id_type=pl.DeviceIdType.MESH,
        ).start()
        return carry

    lax.fori_loop(1, total, spread, 0)
    others = gall.at[pl.ds(0, total - 1)]
    pltpu.make_async_copy(others, others, grsem).wait()
    pltpu.make_async_copy(others, others, gssem).wait()
    whole = jnp.sum(gall[...], axis=0)
    splat[...] = jnp.broadcast_to(whole, splat.shape).T

    def entry(i, j):
        row = pair_index(i, j)
        return splat[row : row + 1, :]

    solved, worst = gram_solve(entry, ITERS)
    flag[...] = jnp.broadcast_to(worst, flag.shape)

    def combine(x, carry):
        vector = []
        for f in range(fields):
            item = solved[0] * basis[0, f, x]
            for k in range(1, ITERS):
                item = item + solved[k] * basis[k, f, x]
            vector.append(item)
        found = precondition(x, vector)
        for f in range(fields):
            out[f, x] = found[f]
        return carry

    lax.fori_loop(0, nx, combine, 0)


def fused(sizes, residual, reaction, transport, congestion):
    levels, nx, ny, nz = reaction.shape
    fields = 2 * levels
    total = sizes[0] * sizes[1] * sizes[2]
    pairs = pair_index(ITERS, ITERS) + 1
    assert fields * nx <= nz and pairs <= nz and nx % PLANES == 0
    f32 = jnp.float32
    hbm = pl.BlockSpec(memory_space=pl.ANY)
    vmem = pl.BlockSpec(memory_space=pltpu.VMEM)
    out, flag = pl.pallas_call(
        functools.partial(kernel, levels, sizes),
        out_shape=(
            jax.ShapeDtypeStruct((fields, nx, ny, nz), f32),
            jax.ShapeDtypeStruct((8, nz), f32),
        ),
        in_specs=[hbm] * 4,
        out_specs=(vmem, vmem),
        scratch_shapes=[
            pltpu.VMEM((ITERS + 1, fields, nx, ny, nz), f32),
            pltpu.VMEM((levels, nx, ny, nz), f32),
            pltpu.VMEM((levels, nx, ny, nz), f32),
            pltpu.VMEM((levels, nx, ny, nz), f32),
            pltpu.VMEM((2, fields, nx, ny, nz), f32),
            pltpu.VMEM((2, 2, fields, ny, nz), f32),
            pltpu.VMEM((2, 2, fields, nx, nz), f32),
            pltpu.VMEM((2, 2, fields, nx, nz), f32),
            pltpu.VMEM((2, 2, ny, nz), f32),
            pltpu.VMEM((2, 2, ny, nz), f32),
            pltpu.VMEM((nz, nz), f32),
            pltpu.VMEM((nz, nz), f32),
            pltpu.VMEM((1, nz), f32),
            pltpu.VMEM((total, 1, nz), f32),
            pltpu.SemaphoreType.DMA((4,)),
            pltpu.SemaphoreType.DMA((3, 2, 2)),
            pltpu.SemaphoreType.DMA((3, 2, 2)),
            pltpu.SemaphoreType.DMA,
            pltpu.SemaphoreType.DMA,
        ],
        compiler_params=pltpu.CompilerParams(
            collective_id=0, has_side_effects=True, vmem_limit_bytes=40 * 1024 * 1024
        ),
        name="krylov",
    )(residual.reshape((fields, nx, ny, nz)), reaction, transport, congestion)
    return out.reshape(residual.shape), flag


def neighbours(field):
    total = 0.0
    for axis, dim in (("gx", 2), ("gy", 3), ("gz", 4)):
        count = lax.axis_size(axis)
        size = field.shape[dim]
        forward = [(i, i + 1) for i in range(count - 1)]
        backward = [(target, source) for source, target in forward]
        low = lax.ppermute(lax.slice_in_dim(field, size - 1, size, axis=dim), axis, forward)
        high = lax.ppermute(lax.slice_in_dim(field, 0, 1, axis=dim), axis, backward)
        below = jnp.concatenate([low, lax.slice_in_dim(field, 0, size - 1, axis=dim)], dim)
        above = jnp.concatenate([lax.slice_in_dim(field, 1, size, axis=dim), high], dim)
        total = total + below + above
    return total


def jacobian(vector, reaction, transport, congestion):
    lapped = 6.0 * vector - neighbours(vector)
    value_part, density_part = (vector[0], vector[1])
    later = jnp.concatenate([value_part[1:], jnp.zeros_like(value_part[:1])], 0)
    earlier = jnp.concatenate([jnp.zeros_like(density_part[:1]), density_part[:-1]], 0)
    first = (
        time_rate * (value_part - later)
        + lapped[0]
        + reaction * value_part
        - congestion * density_part
    )
    second = (
        time_rate * (density_part - earlier)
        + lapped[1]
        + reaction * density_part
        - transport * lapped[0]
    )
    return jnp.stack([first, second], 0)


def precondition(vector, reaction, transport):
    levels = vector.shape[1]
    diag = time_rate + 6.0 + reaction
    value_levels = [None] * levels
    carry = jnp.zeros_like(vector[0, 0])
    for level in range(levels - 1, -1, -1):
        carry = (vector[0, level] + time_rate * carry) / diag[level]
        value_levels[level] = carry
    density_levels = []
    carry = jnp.zeros_like(vector[1, 0])
    for level in range(levels):
        carry = (
            vector[1, level] + time_rate * carry + 6.0 * transport[level] * value_levels[level]
        ) / diag[level]
        density_levels.append(carry)
    return jnp.stack([jnp.stack(value_levels, 0), jnp.stack(density_levels, 0)], 0)


def arnoldi(residual, reaction, transport, congestion):
    dims = tuple(range(1, residual.ndim + 1))
    beta = jnp.sqrt(lax.psum(jnp.sum(residual * residual), AXES))
    basis = jnp.zeros((ITERS + 1,) + residual.shape, residual.dtype).at[0].set(residual / beta)
    heights = jnp.zeros((ITERS, ITERS + 1), residual.dtype)

    def step(c, state):
        basis, heights = state
        search = precondition(basis[c], reaction, transport)
        image = jacobian(search, reaction, transport, congestion)
        coeffs = lax.psum(jnp.sum(basis * image[None], axis=dims), AXES)
        image = image - jnp.sum(coeffs.reshape((-1,) + (1,) * residual.ndim) * basis, axis=0)
        height = jnp.sqrt(lax.psum(jnp.sum(image * image), AXES))
        basis = basis.at[c + 1].set(image / height)
        return basis, heights.at[c].set(coeffs.at[c + 1].set(height))

    basis, heights = lax.fori_loop(0, ITERS, step, (basis, heights))
    columns = [[heights[c, i] for i in range(c + 2)] for c in range(ITERS)]
    solved = least_squares(columns, beta, ITERS)
    mixed = sum(solved[c] * basis[c] for c in range(ITERS))
    return precondition(mixed, reaction, transport)


def body(sizes, residual_in, reaction, transport, congestion):
    update, flag = fused(sizes, residual_in, reaction, transport, congestion)
    return lax.cond(
        flag[0, 0] > PIVOT,
        lambda update, *rest: update,
        lambda update, *rest: arnoldi(*rest),
        update, residual_in, reaction, transport, congestion,
    )


def solution(mesh):
    placed = (
        P(None, None, "gx", "gy", "gz"),
        P(None, "gx", "gy", "gz"),
        P(None, "gx", "gy", "gz"),
        P(None, "gx", "gy", "gz"),
    )
    sizes = tuple(mesh.shape[axis] for axis in AXES)
    return jax.shard_map(
        functools.partial(body, sizes), mesh=mesh, in_specs=placed,
        out_specs=P(None, None, "gx", "gy", "gz"), check_vma=False,
    )
```

profile of v0, /device:TPU:0, one launch (start us, length us, event | category | flops | bytes accessed | tf_op | source)
XLA Modules:
  0.0 53.9 jit_solution(5221268720466952364)
XLA Ops:
  0.0 50.2 %krylov.1 = (f32[8,16,16,128]{3,2,1,0:T(8,128)}, f32[8,128]{1,0:T(8,128)S(1)}) custom-call(f32[8,16,16,128]{3,2,1,0:T(8,128)} %bitcast.256, f32[4,16,16,128]{3,2,1,0:T(8,128)} %reaction.1, f32[4,16,16,128]{3,2,1,0:T(8,128)} %transport.1, f32[4,16,16,128]{3,2,1,0:T(8,128)} %congestion.1), custom_call_target="tpu_custom_call" | custom-call | tf_op jit(solution)/shard_map/krylov/pallas_call | solution.py:387
  50.2 0.5 slice.663
  51.4 0.2 conditional.1
  51.6 2.3 %copy.48 = f32[2,4,16,16,128]{4,3,2,1,0:T(8,128)} copy(f32[2,4,16,16,128]{4,3,2,1,0:T(8,128)} %get-tuple-element.260) | data formatting | bytes 2097152
where the time goes:
time: 54.1 us; the launch traced here: 53.9 us
  Pallas kernels  50.2 us (93%)
  local copies, waits for them, and re-layouts  2.78 us (5%)
  between operations  0.67 us (1%)
    pallas_call x1, Pallas kernels, fused(): pl.pallas_call(functools.partial(kernel, levels, sizes), out_shape=(jax.S...  50.2 us
    unnamed x1, local copies, waits for them, and re-layouts  2.27 us

commit v1 on v0

v1 whole, which is shorter than its diff:
```python
import functools

import jax
import jax.numpy as jnp
from jax import lax
from jax.experimental import pallas as pl
from jax.experimental.pallas import tpu as pltpu
from jax.sharding import PartitionSpec as P

ITERS = 8
AXES = ("gx", "gy", "gz")
time_rate = 1.0
SCALE = 2.5
BACK = 1.0
PIVOT = 2.5e-3
PLANES = 4
PAD = 8
FIRST_BACK = 2
GROUP = 3
SPAN = 2
STARTS = ("x0", "y0", "gx", "gy")
CHANNELS = {
    "x": (8, 2, ITERS),
    "y": (24, 2, 4),
    "c": (32, 4, 4),
    ("z", 0): (48, 2, 2),
    ("z", 1): (52, 2, 4),
    ("z", 2): (60, 2, 2),
}


def gram_row(row, column):
    return column * (ITERS + 1) + row


def least_squares(columns, beta, steps):
    zero = jnp.zeros_like(beta)
    rotations = []
    target = [beta] + [zero] * steps
    upper = []
    for column_index in range(steps):
        column = list(columns[column_index])
        for place, (cosine, sine) in enumerate(rotations):
            upper_entry = cosine * column[place] + sine * column[place + 1]
            lower_entry = -sine * column[place] + cosine * column[place + 1]
            column[place], column[place + 1] = (upper_entry, lower_entry)
        radius = jnp.sqrt(column[column_index] ** 2 + column[column_index + 1] ** 2)
        inverse = 1.0 / radius
        cosine = column[column_index] * inverse
        sine = column[column_index + 1] * inverse
        column[column_index] = inverse
        rotations.append((cosine, sine))
        target[column_index], target[column_index + 1] = (
            cosine * target[column_index],
            -sine * target[column_index],
        )
        upper.append(column[: column_index + 1])
    solved = [None] * steps
    for row_index in range(steps - 1, -1, -1):
        accum = target[row_index]
        for later_index in range(steps - 1, row_index, -1):
            accum = accum - upper[later_index][row_index] * solved[later_index]
        solved[row_index] = accum * upper[row_index][row_index]
    return solved


def gram_solve(gram, steps):
    size = steps + 1
    work = {(i, j): gram(i, j) for j in range(size) for i in range(j + 1)}
    factor = {}
    worst = None
    for i in range(size):
        ratio = work[i, i] / gram(i, i)
        worst = ratio if worst is None else jnp.where(ratio > worst, worst, ratio)
        pivot = jnp.sqrt(work[i, i])
        inverse = 1.0 / pivot
        factor[i, i] = pivot
        for j in range(i + 1, size):
            factor[i, j] = work[i, j] * inverse
        for a in range(i + 1, size):
            for b in range(a, size):
                work[a, b] = work[a, b] - factor[i, a] * factor[i, b]
    columns = []
    for k in range(steps):
        column = []
        for i in range(k + 2):
            entry = -factor[i, k + 1] * (1.0 / SCALE)
            if i <= k:
                entry = entry + factor[i, k]
            if k >= FIRST_BACK and i <= k - 1:
                entry = entry - factor[i, k - 1] * (BACK / SCALE)
            column.append(entry)
        columns.append(column)
    return least_squares(columns, factor[0, 0], steps), worst


def kernel(
    levels, sizes, residual, reaction, transport, congestion, out, flag,
    basis, coef, inv, search, beside, xin, yin, yout, rows, cin, cout, zin, zout,
    ghost_x, ghost_y, ghost_inv, given, past, mixer, zsum, zside, gram, splat, gsend, gall,
    insem, ssem, rsem, gssem, grsem,
):
    fields = 2 * levels
    nx, ny, nz = residual.shape[1:]
    total = sizes[0] * sizes[1] * sizes[2]
    index = [lax.axis_index(axis) for axis in AXES]
    me = (index[0] * sizes[1] + index[1]) * sizes[2] + index[2]
    lane = lax.broadcasted_iota(jnp.int32, (ny, nz), 1)
    plane = pl.ds(0, ny)
    next_lane = (lane + 1) & (nz - 1)
    ends_mask = jnp.logical_or(lane == 0, lane == nz - 1)
    own = pl.ds(PAD, ny)
    blank = jnp.zeros((ny, nz), jnp.float32)
    weight, couple = coef.at[1], coef.at[2]

    loads = [
        pltpu.make_async_copy(src, dst, insem.at[place])
        for place, (src, dst) in enumerate((
            (residual, basis.at[1, :, pl.ds(0, nx), pl.ds(0, ny)]), (reaction, coef.at[0]),
            (transport, coef.at[1]), (congestion, coef.at[2]),
        ))
    ]
    for load in loads:
        load.start()

    for buffer in (xin, yin, cin, zin, ghost_x, ghost_y):
        buffer[...] = jnp.zeros_like(buffer)
    for slot in range(2):
        edge = nx + 1 if slot else 0
        search[0, :, edge] = jnp.zeros_like(search[0, :, edge])
    beside[0] = jnp.zeros_like(beside[0])
    past[...] = jnp.zeros_like(past)
    basis[0] = jnp.zeros_like(basis[0])
    gram[...] = jnp.zeros_like(gram)

    def ident(other):
        return (other // (sizes[1] * sizes[2]), (other // sizes[2]) % sizes[1], other % sizes[2])

    barrier = pltpu.get_barrier_semaphore()

    def greet(step, carry):
        pl.semaphore_signal(
            barrier, inc=1, device_id=ident((me + step) % total),
            device_id_type=pl.DeviceIdType.MESH,
        )
        return carry

    lax.fori_loop(1, total, greet, 0)

    def reaches(shift):
        ok = None
        for axis, move in enumerate(shift):
            if move == 0:
                continue
            this = index[axis] < sizes[axis] - 1 if move > 0 else index[axis] > 0
            ok = this if ok is None else jnp.logical_and(ok, this)
        return ok

    def remote(src, dst, place, shift):
        return pltpu.make_async_remote_copy(
            src_ref=src, dst_ref=dst, send_sem=ssem, recv_sem=rsem.at[place],
            device_id=tuple(i + move for i, move in zip(index, shift)),
            device_id_type=pl.DeviceIdType.MESH,
        )

    def number(key):
        kind, rest = key[0], key[1:]
        if kind in STARTS:
            return 2 * STARTS.index(kind) + rest[0]
        base, width, cycle = CHANNELS[kind if kind != "z" else (kind, rest[1])]
        spot = 0
        for part in rest[2 if kind == "z" else 1 :]:
            spot = 2 * spot + part
        return base + lax.rem(rest[0], cycle) * width + spot

    def start(key, src, dst, shift, wanted=None):
        go = reaches(shift)

        @pl.when(go if wanted is None else jnp.logical_and(go, wanted))
        def _():
            remote(src, dst, number(key), shift).start()

    def arrive(key, dst, shift):
        @pl.when(reaches([-move for move in shift]))
        def _():
            remote(dst, dst, number(key), shift).wait_recv()

    def drain(key, src, shift, wanted=None):
        go = reaches(shift)

        @pl.when(go if wanted is None else jnp.logical_and(go, wanted))
        def _():
            remote(src, src, number(key), shift).wait_send()

    def along(axis, side):
        shift = [0, 0, 0]
        shift[axis] = 1 if side == 0 else -1
        return shift

    def x_plane(near, side):
        return nx - near if side == 0 else 1 + near

    def send_x(k, wanted=None):
        for side in range(2):
            start(("x", k, side), search.at[k, :, x_plane(1, side), own],
                  xin.at[k, side], along(0, side), wanted)

    def send_y(k, wanted=None):
        for side in range(2):
            start(("y", k, side), yout.at[k, side], yin.at[k, side], along(1, side), wanted)

    def send_c(k, wanted=None):
        for cx in range(2):
            for cy in range(2):
                shift = [1 - 2 * cx, 1 - 2 * cy, 0]
                start(("c", k, cx, cy), cout.at[k, cx, cy], cin.at[k, cx, cy], shift, wanted)

    def send_z(k, kind, packs, wanted=None):
        for side in range(2):
            zout[k, kind, side] = packs[side]
            start(("z", k, kind, side), zout.at[k, kind, side], zin.at[k, kind, side],
                  along(2, side), wanted)

    def take_x(k):
        for side in range(2):
            arrive(("x", k, side), xin.at[k, side], along(0, side))

    def take_y(k):
        for side in range(2):
            arrive(("y", k, side), yin.at[k, side], along(1, side))

    def take_c(k):
        for cx in range(2):
            for cy in range(2):
                arrive(("c", k, cx, cy), cin.at[k, cx, cy], [1 - 2 * cx, 1 - 2 * cy, 0])

    def take_z(k, kind):
        for side in range(2):
            arrive(("z", k, kind, side), zin.at[k, kind, side], along(2, side))

    def precondition(scale, mass, vector):
        value, density = [None] * levels, [None] * levels
        carry = None
        for t in range(levels - 1, -1, -1):
            carry = vector[t] if carry is None else vector[t] + carry
            carry = carry * scale(t)
            value[t] = carry
        carry = None
        for t in range(levels):
            push = vector[levels + t] + (6.0 * mass(t)) * value[t]
            carry = push if carry is None else push + carry
            carry = carry * scale(t)
            density[t] = carry
        return value + density

    def mix(founds):
        blends = []
        for odd in range(2):
            whole = jnp.concatenate([found[f] for found in founds for f in range(odd, fields, 2)], 0)
            high = whole.astype(jnp.bfloat16)
            low = (whole - high.astype(jnp.float32)).astype(jnp.bfloat16)
            blends.append(jnp.dot(
                jnp.concatenate([high, low], 1), mixer[odd], preferred_element_type=jnp.float32
            ))
        mixed = []
        for place in range(len(founds)):
            parts = []
            for f in range(fields):
                row = (place * (fields // 2) + f // 2) * ny
                parts.append((blends[f % 2][row : row + ny, :nz], blends[f % 2][row : row + ny, nz:]))
            mixed.append(parts)
        return mixed

    def pack(packs, base, mixed):
        high, low = packs
        for f in range(fields):
            place = base + f
            high = jnp.where(lane == place, mixed[f][1], high)
            low = jnp.where(next_lane == place, mixed[f][1], low)
        return high, low

    def advance(k, kind, base, center, low, high, below, above, beyond, mass, pull, prior):
        zlow, zhigh = zin.at[k, kind, 0], zin.at[k, kind, 1]

        def around(f):
            place = base + f
            edge = jnp.where(lane == place, zlow[...], zhigh[...])
            edge = jnp.where(ends_mask, pltpu.roll(edge, (nz - place) & (nz - 1), 1), 0.0)
            return ((below(f) + above(f)) + (low(f) + high(f))) + (beyond(f) + edge)

        found = [None] * fields
        for t in range(levels):
            value = around(t)
            density = around(levels + t) - mass(t) * value
            value = value + pull(t) * center(levels + t)
            for f, item in ((t, value), (levels + t, density)):
                found[f] = SCALE * item - BACK * prior(f)
        return found

    def publish(k, x, found, fixed):
        for f in range(fields):
            search[k, f, x + 1, own] = found[f]
            for side, (edge, near) in enumerate(((0, ny - 2), (ny - 1, 1))):
                rows[k, side, f, pl.ds(x, 1), :] = found[f][edge : edge + 1, :]
                yout[k, side, f, pl.ds(x, 1), :] = found[f][near : near + 1, :]
            if fixed is not None:
                for cy in range(2):
                    edge = ny - 1 if cy == 0 else 0
                    cout[k, fixed, cy, f : f + 1, :] = found[f][edge : edge + 1, :]

    def own_planes(k, planes, packs):
        before = k * lax.div(lax.div(k, 2) + ITERS - 2, ITERS - 1)
        founds = []
        for x, fixed in planes:
            vector = advance(
                k, 0, x * fields,
                lambda f: search[k, f, x + 1, own],
                lambda f: search[k, f, x + 1, pl.ds(PAD - 1, ny)],
                lambda f: search[k, f, x + 1, pl.ds(PAD + 1, ny)],
                lambda f: search[k, f, x, own],
                lambda f: search[k, f, x + 2, own],
                lambda f: zsum[lax.rem(k, 2), f, x + 1],
                lambda t: weight[t, x],
                lambda t: couple[t, x],
                lambda f: basis[before, f, x, plane],
            )
            for f in range(fields):
                basis[k + 2, f, x, plane] = vector[f]
            founds.append(
                precondition(lambda t: inv[t, x], lambda t: weight[t, x], vector)
            )
        return spread(k + 1, planes, founds, packs)

    def spread(k, planes, founds, packs):
        for (x, fixed), found, mixed in zip(planes, founds, mix(founds)):
            packs = pack(packs, x * fields, mixed)
            publish(k, x, found, fixed)
            for f in range(fields):
                zsum[lax.rem(k, 2), f, x + 1] = mixed[f][0]
        return packs

    def scatter(k, side, get):
        row = PAD - 1 if side == 0 else PAD + ny
        for f in range(fields):
            found = get(f)
            for x in range(nx):
                search[k, f, x + 1, row : row + 1, :] = found[x : x + 1, :]

    def aside(k, side, found, packs):
        mixed = mix([found])[0]
        for f in range(fields):
            zside[lax.rem(k, 2), side, f] = mixed[f][0]
        return pack(packs, side * fields, mixed)

    def across(k, side, edge, found, packs):
        mixed = mix([found])[0]
        for f in range(fields):
            zsum[lax.rem(k, 2), f, edge] = mixed[f][0]
        return pack(packs, side * fields, mixed)

    def y_given():
        packs = (blank, blank)
        for side in range(2):
            arrive(("y0", side), beside.at[0, side, :, own], along(1, side))
        for side in range(2):
            found = [beside[0, side, f, own] for f in range(fields)]
            scatter(0, side, lambda f: found[f])
            packs = aside(0, side, found, packs)
        send_z(0, 1, packs)
        for axis, ghost in enumerate((ghost_x, ghost_y)):
            for side in range(2):
                arrive(("gx" if axis == 0 else "gy", side), ghost.at[side], along(axis, side))
                there = index[axis] > 0 if side == 0 else index[axis] < sizes[axis] - 1
                for t in range(levels):
                    ghost_inv[axis, side, t] = jnp.where(
                        there, 1.0 / (time_rate + 6.0 + ghost[side, 0, t]), 0.0
                    )

    def y_ghosts(k):
        packs = (blank, blank)
        j = k - 1
        take_y(j)
        take_c(j)
        take_z(j, 1)
        for side in range(2):
            for f in range(fields):
                beside[j, side, f, PAD - 1 : PAD, :] = cin[j, 0, side, f : f + 1, :]
                beside[j, side, f, PAD + nx : PAD + nx + 1, :] = cin[j, 1, side, f : f + 1, :]
            vector = advance(
                j, 1, side * fields,
                lambda f: beside[j, side, f, own],
                lambda f: beside[j, side, f, pl.ds(PAD - 1, nx)],
                lambda f: beside[j, side, f, pl.ds(PAD + 1, nx)],
                lambda f: yin[j, side, f],
                lambda f: rows[j, side, f],
                lambda f: zside[lax.rem(j, 2), side, f],
                lambda t: ghost_y[side, 1, t],
                lambda t: ghost_y[side, 2, t],
                lambda f: past[lax.rem(k, 2), 1, side, f],
            )
            for f in range(fields):
                past[lax.rem(k, 2), 1, side, f] = vector[f]
            found = precondition(
                lambda t: ghost_inv[1, side, t], lambda t: ghost_y[side, 1, t], vector
            )
            for f in range(fields):
                beside[k, side, f, own] = found[f]
            scatter(k, side, lambda f: found[f])
            packs = aside(k, side, found, packs)
        send_z(k, 1, packs, k < ITERS - 1)

    def x_given():
        packs = (blank, blank)
        for side in range(2):
            edge = nx + 1 if side else 0
            arrive(("x0", side), search.at[0, :, edge, own], along(0, side))
            found = [search[0, f, edge, own] for f in range(fields)]
            packs = across(0, side, edge, found, packs)
        send_z(0, 2, packs)

    def x_ghosts(k):
        packs = (blank, blank)
        j = k - 1
        take_x(j)
        take_z(j, 2)
        for side in range(2):
            edge, inner = (0, 1) if side == 0 else (nx + 1, nx)
            for f in range(fields):
                search[j, f, edge, PAD - 1 : PAD, :] = cin[j, side, 0, f : f + 1, :]
                search[j, f, edge, PAD + ny : PAD + ny + 1, :] = cin[j, side, 1, f : f + 1, :]
            vector = advance(
                j, 2, side * fields,
                lambda f: search[j, f, edge, own],
                lambda f: search[j, f, edge, pl.ds(PAD - 1, ny)],
                lambda f: search[j, f, edge, pl.ds(PAD + 1, ny)],
                lambda f: xin[j, side, f],
                lambda f: search[j, f, inner, own],
                lambda f: zsum[lax.rem(j, 2), f, edge],
                lambda t: ghost_x[side, 1, t],
                lambda t: ghost_x[side, 2, t],
                lambda f: past[lax.rem(k, 2), 0, side, f],
            )
            for f in range(fields):
                past[lax.rem(k, 2), 0, side, f] = vector[f]
            found = precondition(
                lambda t: ghost_inv[0, side, t], lambda t: ghost_x[side, 1, t], vector
            )
            for f in range(fields):
                search[k, f, edge, own] = found[f]
            packs = across(k, side, edge, found, packs)
        send_z(k, 2, packs, k < ITERS - 1)

    def dots(k):
        def group(g, carry):
            def step(place, accs):
                sums = [[] for _ in range(GROUP)]
                for x in range(SPAN):
                    x = place * SPAN + x
                    mine = [basis[k + 1, f, x, plane] for f in range(fields)]
                    for i in range(GROUP):
                        terms = [mine[f] * basis[g * GROUP + i + 1, f, x, plane] for f in range(fields)]
                        while len(terms) > 1:
                            terms = [a + b for a, b in zip(terms[::2], terms[1::2])]
                        sums[i].append(terms[0])
                return tuple(acc + sum(more) for acc, more in zip(accs, sums))

            accs = lax.fori_loop(0, nx // SPAN, step, (blank,) * GROUP)
            for i in range(GROUP):
                row = gram_row(g * GROUP + i, k)
                gram[pl.ds(row, 1), :] = jnp.sum(accs[i], axis=0, keepdims=True)
            return carry

        lax.fori_loop(0, lax.div(k, GROUP) + 1, group, 0)

    for load in loads:
        load.wait()

    def invert(x, carry):
        for t in range(levels):
            inv[t, x] = 1.0 / (time_rate + 6.0 + coef[0, t, x])
            for which in range(3):
                item = coef[which, t, x]
                given[0, which, t, pl.ds(x, 1), :] = item[ny - 1 : ny, :]
                given[1, which, t, pl.ds(x, 1), :] = item[0:1, :]
        return carry

    lax.fori_loop(0, nx, invert, 0)
    def first(planes, packs):
        founds = [
            precondition(
                lambda t: inv[t, x], lambda t: weight[t, x],
                [basis[1, f, x, plane] for f in range(fields)],
            )
            for x, _ in planes
        ]
        return spread(0, planes, founds, packs)

    def sweep(body, packs, low):
        return lax.fori_loop(
            0, (nx - 2 * low) // PLANES,
            lambda step, packs: body(
                [(low + step * PLANES + place, None) for place in range(PLANES)], packs
            ),
            packs,
        )

    pl.semaphore_wait(barrier, total - 1)
    for side in range(2):
        start(("gx", side), coef.at[:, :, nx - 1 if side == 0 else 0], ghost_x.at[side],
              along(0, side))
    for side in range(2):
        start(("gy", side), given.at[side], ghost_y.at[side], along(1, side))
    from_lane = lax.broadcasted_iota(jnp.int32, (2 * nz, 2 * nz), 0) & (nz - 1)
    to_lane = lax.broadcasted_iota(jnp.int32, (2 * nz, 2 * nz), 1)
    for odd in range(2):
        beside_lane = jnp.logical_or(from_lane - to_lane == 1, to_lane - from_lane == 1)
        last_lane = jnp.logical_and((to_lane & 1) == odd, from_lane == nz - 1)
        first_lane = jnp.logical_and((to_lane & 1) != odd, from_lane == 0)
        taken = jnp.where(
            to_lane < nz, beside_lane.astype(jnp.int32),
            jnp.logical_or(last_lane, first_lane).astype(jnp.int32),
        )
        mixer[odd] = taken.astype(jnp.float32).astype(jnp.bfloat16)
    ends = [(0, 1), (nx - 1, 0)]
    packs = first(ends, (blank, blank))
    packs = first([(1, None), (nx - 2, None)], packs)
    packs = sweep(first, packs, 2)
    for side in range(2):
        start(("x0", side), search.at[0, :, nx if side == 0 else 1, own],
              search.at[0, :, nx + 1 if side else 0, own], along(0, side))
    for side in range(2):
        start(("y0", side), rows.at[0, 1 - side], beside.at[0, side, :, own], along(1, side))
    send_z(0, 0, packs)
    send_c(0)
    send_x(0)
    send_y(0)
    dots(0)
    y_given()

    def iterate(k, carry):
        more = k < ITERS - 2

        @pl.when(k > 0)
        def _():
            y_ghosts(k)

        take_z(k, 0)
        body = functools.partial(own_planes, k)
        packs = body([(1, None), (nx - 2, None)], (blank, blank))
        send_x(k + 1, more)
        packs = sweep(body, packs, 2)

        @pl.when(k == 0)
        def _():
            x_given()

        @pl.when(k > 0)
        def _():
            x_ghosts(k)

        packs = body(ends, packs)
        send_z(k + 1, 0, packs, k < ITERS - 1)
        send_c(k + 1, more)
        send_y(k + 1, more)
        dots(k + 1)
        return carry

    lax.fori_loop(0, ITERS, iterate, 0)

    def settle(k, carry):
        more = k < ITERS - 1
        for side in range(2):
            drain(("x", k, side), xin.at[k, side], along(0, side), more)
            drain(("y", k, side), yin.at[k, side], along(1, side), more)
            for cy in range(2):
                drain(("c", k, side, cy), cin.at[k, side, cy], [1 - 2 * side, 1 - 2 * cy, 0], more)
            for kind in range(3):
                drain(("z", k, kind, side), zin.at[k, kind, side], along(2, side),
                      None if kind == 0 else more)
        return carry

    lax.fori_loop(0, ITERS, settle, 0)
    for side in range(2):
        drain(("x0", side), search.at[0, :, 0, own], along(0, side))
        drain(("y0", side), beside.at[0, side, :, own], along(1, side))
        drain(("gx", side), ghost_x.at[side], along(0, side))
        drain(("gy", side), ghost_y.at[side], along(1, side))

    local = jnp.sum(gram[...].T, axis=0, keepdims=True)
    gsend[...] = local
    gall[me] = local

    def spread(step, carry):
        pltpu.make_async_remote_copy(
            src_ref=gsend, dst_ref=gall.at[me], send_sem=gssem, recv_sem=grsem,
            device_id=ident((me + step) % total), device_id_type=pl.DeviceIdType.MESH,
        ).start()
        return carry

    lax.fori_loop(1, total, spread, 0)
    others = gall.at[pl.ds(0, total - 1)]
    pltpu.make_async_copy(others, others, grsem).wait()
    pltpu.make_async_copy(others, others, gssem).wait()
    whole = jnp.sum(gall[...], axis=0)
    splat[...] = jnp.broadcast_to(whole, splat.shape).T

    def entry(i, j):
        row = gram_row(i, j)
        return splat[row : row + 1, :]

    solved, worst = gram_solve(entry, ITERS)
    flag[...] = jnp.broadcast_to(worst, flag.shape)

    def combine(x, carry):
        for f in range(fields):
            item = solved[0] * search[0, f, x + 1, own]
            for k in range(1, ITERS):
                item = item + solved[k] * search[k, f, x + 1, own]
            out[f, x] = item
        return carry

    lax.fori_loop(0, nx, combine, 0)


def fused(sizes, residual, reaction, transport, congestion):
    levels, nx, ny, nz = reaction.shape
    fields = 2 * levels
    total = sizes[0] * sizes[1] * sizes[2]
    pairs = (ITERS + 1) ** 2
    assert (ITERS + 1) % GROUP == 0
    assert fields * nx <= nz and pairs <= nz and (nx - 4) % PLANES == 0 and nx == ny
    assert nz & (nz - 1) == 0
    f32 = jnp.float32
    hbm = pl.BlockSpec(memory_space=pl.ANY)
    vmem = pl.BlockSpec(memory_space=pltpu.VMEM)
    wide = ny + 3 * PAD
    copies = sum(width * cycle for _, width, cycle in CHANNELS.values()) + 2 * len(STARTS)
    out, flag = pl.pallas_call(
        functools.partial(kernel, levels, sizes),
        out_shape=(
            jax.ShapeDtypeStruct((fields, nx, ny, nz), f32),
            jax.ShapeDtypeStruct((8, nz), f32),
        ),
        in_specs=[hbm] * 4,
        out_specs=(vmem, vmem),
        scratch_shapes=[
            pltpu.VMEM((ITERS + 2, fields, nx + 1, ny + PAD, nz), f32),
            pltpu.VMEM((3, levels, nx, ny, nz), f32),
            pltpu.VMEM((levels, nx, ny, nz), f32),
            pltpu.VMEM((ITERS + 1, fields, nx + 2, wide, nz), f32),
            pltpu.VMEM((ITERS, 2, fields, wide, nz), f32),
            pltpu.VMEM((ITERS + 1, 2, fields, ny, nz), f32),
            pltpu.VMEM((ITERS + 1, 2, fields, nx, nz), f32),
            pltpu.VMEM((ITERS + 1, 2, fields, nx, nz), f32),
            pltpu.VMEM((ITERS + 1, 2, fields, nx, nz), f32),
            pltpu.VMEM((ITERS + 1, 2, 2, fields, nz), f32),
            pltpu.VMEM((ITERS + 1, 2, 2, fields, nz), f32),
            pltpu.VMEM((ITERS + 1, 3, 2, ny, nz), f32),
            pltpu.VMEM((ITERS + 1, 3, 2, ny, nz), f32),
            pltpu.VMEM((2, 3, levels, ny, nz), f32),
            pltpu.VMEM((2, 3, levels, nx, nz), f32),
            pltpu.VMEM((2, 2, levels, ny, nz), f32),
            pltpu.VMEM((2, 3, levels, nx, nz), f32),
            pltpu.VMEM((2, 2, 2, fields, ny, nz), f32),
            pltpu.VMEM((2, 2 * nz, 2 * nz), jnp.bfloat16),
            pltpu.VMEM((2, fields, nx + 2, ny, nz), f32),
            pltpu.VMEM((2, 2, fields, nx, nz), f32),
            pltpu.VMEM((nz, nz), f32),
            pltpu.VMEM((nz, nz), f32),
            pltpu.VMEM((1, nz), f32),
            pltpu.VMEM((total, 1, nz), f32),
            pltpu.SemaphoreType.DMA((4,)),
            pltpu.SemaphoreType.DMA,
            pltpu.SemaphoreType.DMA((copies,)),
            pltpu.SemaphoreType.DMA,
            pltpu.SemaphoreType.DMA,
        ],
        compiler_params=pltpu.CompilerParams(
            collective_id=0, has_side_effects=True, vmem_limit_bytes=60 * 1024 * 1024
        ),
        name="krylov",
    )(residual.reshape((fields, nx, ny, nz)), reaction, transport, congestion)
    return out.reshape(residual.shape), flag


def neighbours(field):
    total = 0.0
    for axis, dim in (("gx", 2), ("gy", 3), ("gz", 4)):
        count = lax.axis_size(axis)
        size = field.shape[dim]
        forward = [(i, i + 1) for i in range(count - 1)]
        backward = [(target, source) for source, target in forward]
        low = lax.ppermute(lax.slice_in_dim(field, size - 1, size, axis=dim), axis, forward)
        high = lax.ppermute(lax.slice_in_dim(field, 0, 1, axis=dim), axis, backward)
        below = jnp.concatenate([low, lax.slice_in_dim(field, 0, size - 1, axis=dim)], dim)
        above = jnp.concatenate([lax.slice_in_dim(field, 1, size, axis=dim), high], dim)
        total = total + below + above
    return total


def jacobian(vector, reaction, transport, congestion):
    lapped = 6.0 * vector - neighbours(vector)
    value_part, density_part = (vector[0], vector[1])
    later = jnp.concatenate([value_part[1:], jnp.zeros_like(value_part[:1])], 0)
    earlier = jnp.concatenate([jnp.zeros_like(density_part[:1]), density_part[:-1]], 0)
    first = (
        time_rate * (value_part - later)
        + lapped[0]
        + reaction * value_part
        - congestion * density_part
    )
    second = (
        time_rate * (density_part - earlier)
        + lapped[1]
        + reaction * density_part
        - transport * lapped[0]
    )
    return jnp.stack([first, second], 0)


def precondition(vector, reaction, transport):
    levels = vector.shape[1]
    diag = time_rate + 6.0 + reaction
    value_levels = [None] * levels
    carry = jnp.zeros_like(vector[0, 0])
    for level in range(levels - 1, -1, -1):
        carry = (vector[0, level] + time_rate * carry) / diag[level]
        value_levels[level] = carry
    density_levels = []
    carry = jnp.zeros_like(vector[1, 0])
    for level in range(levels):
        carry = (
            vector[1, level] + time_rate * carry + 6.0 * transport[level] * value_levels[level]
        ) / diag[level]
        density_levels.append(carry)
    return jnp.stack([jnp.stack(value_levels, 0), jnp.stack(density_levels, 0)], 0)


def arnoldi(residual, reaction, transport, congestion):
    dims = tuple(range(1, residual.ndim + 1))
    beta = jnp.sqrt(lax.psum(jnp.sum(residual * residual), AXES))
    basis = jnp.zeros((ITERS + 1,) + residual.shape, residual.dtype).at[0].set(residual / beta)
    heights = jnp.zeros((ITERS, ITERS + 1), residual.dtype)

    def step(c, state):
        basis, heights = state
        search = precondition(basis[c], reaction, transport)
        image = jacobian(search, reaction, transport, congestion)
        coeffs = lax.psum(jnp.sum(basis * image[None], axis=dims), AXES)
        image = image - jnp.sum(coeffs.reshape((-1,) + (1,) * residual.ndim) * basis, axis=0)
        height = jnp.sqrt(lax.psum(jnp.sum(image * image), AXES))
        basis = basis.at[c + 1].set(image / height)
        return basis, heights.at[c].set(coeffs.at[c + 1].set(height))

    basis, heights = lax.fori_loop(0, ITERS, step, (basis, heights))
    columns = [[heights[c, i] for i in range(c + 2)] for c in range(ITERS)]
    solved = least_squares(columns, beta, ITERS)
    mixed = sum(solved[c] * basis[c] for c in range(ITERS))
    return precondition(mixed, reaction, transport)


def body(sizes, residual_in, reaction, transport, congestion):
    update, flag = fused(sizes, residual_in, reaction, transport, congestion)
    return lax.cond(
        flag[0, 0] > PIVOT,
        lambda update, *rest: update,
        lambda update, *rest: arnoldi(*rest),
        update, residual_in, reaction, transport, congestion,
    )


def solution(mesh):
    placed = (
        P(None, None, "gx", "gy", "gz"),
        P(None, "gx", "gy", "gz"),
        P(None, "gx", "gy", "gz"),
        P(None, "gx", "gy", "gz"),
    )
    sizes = tuple(mesh.shape[axis] for axis in AXES)
    return jax.shard_map(
        functools.partial(body, sizes), mesh=mesh, in_specs=placed,
        out_specs=P(None, None, "gx", "gy", "gz"), check_vma=False,
    )
```

time: 54.1 us -> 52 us (0.961)
  Pallas kernels: 50.2 us -> 47.4 us
  local copies, waits for them, and re-layouts: 2.78 us -> 3.46 us
    pallas_call x1, Pallas kernels: 50.2 us -> 47.4 us  [fused(): pl.pallas_call(functools.partial(kernel, levels, sizes), out_shape=(jax.S...]
    slice x1, local copies, waits for them, and re-layouts: 0.51 us -> 1.19 us  [body(): flag[0, 0] > PIVOT]
where the time goes in v1:
time: 52 us; the launch traced here: 51.8 us
  Pallas kernels  47.4 us (91%)
  local copies, waits for them, and re-layouts  3.46 us (7%)
  between operations  0.67 us (1%)
    pallas_call x1, Pallas kernels, fused(): pl.pallas_call(functools.partial(kernel, levels, sizes), out_shape=(jax.S...  47.4 us
    unnamed x1, local copies, waits for them, and re-layouts  2.27 us
    slice x1, local copies, waits for them, and re-layouts, body(): flag[0, 0] > PIVOT  1.19 us

profile of v1, /device:TPU:0, one launch (start us, length us, event | category | flops | bytes accessed | tf_op | source)
XLA Modules:
  0.0 51.8 jit_solution(3541742447503997299)
XLA Ops:
  0.0 47.4 %krylov.1 = (f32[8,16,16,128]{3,2,1,0:T(8,128)}, f32[8,128]{1,0:T(8,128)}) custom-call(f32[8,16,16,128]{3,2,1,0:T(8,128)} %bitcast.256, f32[4,16,16,128]{3,2,1,0:T(8,128)} %reaction.1, f32[4,16,16,128]{3,2,1,0:T(8,128)} %transport.1, f32[4,16,16,128]{3,2,1,0:T(8,128)} %congestion.1), custom_call_target="tpu_custom_call" | custom-call | tf_op jit(solution)/shard_map/krylov/pallas_call | solution.py:638
  47.4 1.2 %slice.663 = f32[1,1]{1,0:T(1,128)} slice(f32[8,128]{1,0:T(8,128)} %get-tuple-element.258), slice={[0:1], [0:1]} | slice | bytes 8 | tf_op jit(solution)/shard_map/slice | solution.py:765
  49.3 0.2 conditional.1
  49.5 2.3 %copy.48 = f32[2,4,16,16,128]{4,3,2,1,0:T(8,128)} copy(f32[2,4,16,16,128]{4,3,2,1,0:T(8,128)} %get-tuple-element.260) | data formatting | bytes 2097152

commit v2 on v1

--- a/solution.py
+++ b/solution.py
@@ -17,7 +17,7 @@
 PAD = 8
 FIRST_BACK = 2
 GROUP = 3
-SPAN = 2
+SPAN = 4
 STARTS = ("x0", "y0", "gx", "gy")
 CHANNELS = {
     "x": (8, 2, ITERS),
@@ -98,7 +98,7 @@
     levels, sizes, residual, reaction, transport, congestion, out, flag,
     basis, coef, inv, search, beside, xin, yin, yout, rows, cin, cout, zin, zout,
     ghost_x, ghost_y, ghost_inv, given, past, mixer, zsum, zside, gram, splat, gsend, gall,
-    insem, ssem, rsem, gssem, grsem,
+    ready, insem, ssem, rsem, gssem, grsem, osem,
 ):
     fields = 2 * levels
     nx, ny, nz = residual.shape[1:]
@@ -616,10 +616,12 @@
             item = solved[0] * search[0, f, x + 1, own]
             for k in range(1, ITERS):
                 item = item + solved[k] * search[k, f, x + 1, own]
-            out[f, x] = item
+            ready[f, x] = item
+        pltpu.make_async_copy(ready.at[:, x], out.at[:, x], osem).start()
         return carry
 
     lax.fori_loop(0, nx, combine, 0)
+    pltpu.make_async_copy(ready, out, osem).wait()
 
 
 def fused(sizes, residual, reaction, transport, congestion):
@@ -642,7 +644,7 @@
             jax.ShapeDtypeStruct((8, nz), f32),
         ),
         in_specs=[hbm] * 4,
-        out_specs=(vmem, vmem),
+        out_specs=(hbm, vmem),
         scratch_shapes=[
             pltpu.VMEM((ITERS + 2, fields, nx + 1, ny + PAD, nz), f32),
             pltpu.VMEM((3, levels, nx, ny, nz), f32),
@@ -669,9 +671,11 @@
             pltpu.VMEM((nz, nz), f32),
             pltpu.VMEM((1, nz), f32),
             pltpu.VMEM((total, 1, nz), f32),
+            pltpu.VMEM((fields, nx, ny, nz), f32),
             pltpu.SemaphoreType.DMA((4,)),
             pltpu.SemaphoreType.DMA,
             pltpu.SemaphoreType.DMA((copies,)),
+            pltpu.SemaphoreType.DMA,
             pltpu.SemaphoreType.DMA,
             pltpu.SemaphoreType.DMA,
         ],

time: 52 us -> 52 us (level)
  no operation moved by 1% of the time
where the time goes in v2:
time: 52 us; the launch traced here: 51.8 us
  Pallas kernels  47.4 us (91%)
  local copies, waits for them, and re-layouts  3.46 us (7%)
  between operations  0.67 us (1%)
    pallas_call x1, Pallas kernels, fused(): pl.pallas_call(functools.partial(kernel, levels, sizes), out_shape=(jax.S...  47.4 us
    unnamed x1, local copies, waits for them, and re-layouts  2.27 us
    slice x1, local copies, waits for them, and re-layouts, body(): flag[0, 0] > PIVOT  1.19 us

profile of v2, /device:TPU:0, one launch (start us, length us, event | category | flops | bytes accessed | tf_op | source)
XLA Modules:
  0.0 51.8 jit_solution(9437990733198507710)
XLA Ops:
  0.0 47.4 %krylov.1 = (f32[8,16,16,128]{3,2,1,0:T(8,128)}, f32[8,128]{1,0:T(8,128)}) custom-call(f32[8,16,16,128]{3,2,1,0:T(8,128)} %bitcast.256, f32[4,16,16,128]{3,2,1,0:T(8,128)} %reaction.1, f32[4,16,16,128]{3,2,1,0:T(8,128)} %transport.1, f32[4,16,16,128]{3,2,1,0:T(8,128)} %congestion.1), custom_call_target="tpu_custom_call" | custom-call | tf_op jit(solution)/shard_map/krylov/pallas_call | solution.py:640
  47.4 1.2 %slice.663 = f32[1,1]{1,0:T(1,128)} slice(f32[8,128]{1,0:T(8,128)} %get-tuple-element.258), slice={[0:1], [0:1]} | slice | bytes 8 | tf_op jit(solution)/shard_map/slice | solution.py:769
  49.3 0.2 conditional.1
  49.5 2.3 %copy.48 = f32[2,4,16,16,128]{4,3,2,1,0:T(8,128)} copy(f32[2,4,16,16,128]{4,3,2,1,0:T(8,128)} %get-tuple-element.260) | data formatting | bytes 2097152

commit v3 on v2

--- a/solution.py
+++ b/solution.py
@@ -13,7 +13,7 @@
 SCALE = 2.5
 BACK = 1.0
 PIVOT = 2.5e-3
-PLANES = 4
+PLANES = 6
 PAD = 8
 FIRST_BACK = 2
 GROUP = 3

time: 52 us -> 51.9 us (level)
  no operation moved by 1% of the time
where the time goes in v3:
time: 51.9 us; the launch traced here: 51.7 us
  Pallas kernels  47.3 us (91%)
  local copies, waits for them, and re-layouts  3.46 us (7%)
  between operations  0.67 us (1%)
    pallas_call x1, Pallas kernels, fused(): pl.pallas_call(functools.partial(kernel, levels, sizes), out_shape=(jax.S...  47.3 us
    unnamed x1, local copies, waits for them, and re-layouts  2.27 us
    slice x1, local copies, waits for them, and re-layouts, body(): flag[0, 0] > PIVOT  1.19 us

profile of v3, /device:TPU:0, one launch (start us, length us, event | category | flops | bytes accessed | tf_op | source)
XLA Modules:
  0.0 51.7 jit_solution(1433125280413630103)
XLA Ops:
  0.0 47.3 %krylov.1 = (f32[8,16,16,128]{3,2,1,0:T(8,128)}, f32[8,128]{1,0:T(8,128)}) custom-call(f32[8,16,16,128]{3,2,1,0:T(8,128)} %bitcast.256, f32[4,16,16,128]{3,2,1,0:T(8,128)} %reaction.1, f32[4,16,16,128]{3,2,1,0:T(8,128)} %transport.1, f32[4,16,16,128]{3,2,1,0:T(8,128)} %congestion.1), custom_call_target="tpu_custom_call" | custom-call | tf_op jit(solution)/shard_map/krylov/pallas_call | solution.py:640
  47.3 1.2 %slice.663 = f32[1,1]{1,0:T(1,128)} slice(f32[8,128]{1,0:T(8,128)} %get-tuple-element.258), slice={[0:1], [0:1]} | slice | bytes 8 | tf_op jit(solution)/shard_map/slice | solution.py:769
  49.2 0.2 conditional.1
  49.4 2.3 %copy.48 = f32[2,4,16,16,128]{4,3,2,1,0:T(8,128)} copy(f32[2,4,16,16,128]{4,3,2,1,0:T(8,128)} %get-tuple-element.260) | data formatting | bytes 2097152
